TPU v7x, 128 devices: a whole 4x4x4 slice. The times are simulated.
128 devices in a mesh: ep: 8 (over x, core), fsdp: 16 (over z, y).
Axes of the slice: x: 4, y: 4, z: 4, core: 2. Of those that a mesh axis runs over, the one named last changes fastest.
Arguments:
- master_gate: float32 [128, 2048, 768], P('ep', 'fsdp'), may hold values from -0.1875 to 0.1875
- master_up: float32 [128, 2048, 768], P('ep', 'fsdp'), may hold values from -0.1875 to 0.1875
- router_weight: float32 [2048, 128], P('fsdp', 'ep'), may hold values from -0.125 to 0.125
- router_gain: float32 [2048], P('fsdp'), may hold values from 0.25 to 1.75
Outputs:
- final_gate: bfloat16 [128, 2048, 768], P(('ep', 'fsdp'))
- final_up: bfloat16 [128, 2048, 768], P(('ep', 'fsdp'))
- scale_gate: float32 [128, 768], P(('ep', 'fsdp'))
- scale_up: float32 [128, 768], P(('ep', 'fsdp'))
- serve_router: bfloat16 [2048, 128], replicated
All inputs are finite; a program needn't handle non-finite values.
Results may differ from a plain program's by a relative error of at most 0.001.
Values may be sent and summed in bfloat16 or wider, within the bound.
A program may use at most 128 MiB of HBM per device.

v0:
```python
import jax
import jax.numpy as jnp
from jax import lax
from jax.sharding import Mesh
from jax.sharding import PartitionSpec as P

EP = ("ep_0", "ep_1")
EP_FSDP = ("ep_0", "ep_1", "fsdp")


def copy_for_each(value, axis):
    devices = lax.axis_size(axis)
    return lax.all_to_all(
        jnp.broadcast_to(value[None], (devices, *value.shape)), axis, 0, 0, tiled=True
    )


def taken_together(value, axis):
    return copy_for_each(value, axis).sum(axis=0)


def in_one(arrays, axis):
    ends = [0]
    for a in arrays:
        ends.append(ends[-1] + a.size)
    so_far = taken_together(jnp.concatenate([a.ravel() for a in arrays]), axis)
    return tuple((so_far[b:e].reshape(a.shape) for a, b, e in zip(arrays, ends, ends[1:])))


def sent_together(arrays, axis, split_dim, concat_dim, along):
    ends, at = ([], 0)
    for a in arrays[:-1]:
        at += a.shape[along]
        ends.append(at)
    both = jnp.concatenate(arrays, axis=along)
    return tuple(
        jnp.split(
            lax.all_to_all(both, axis, split_axis=split_dim, concat_axis=concat_dim, tiled=True),
            ends,
            axis=along,
        )
    )


def joined_along(parts, dim):
    dims = list(parts.shape[1:])
    dims[dim] *= parts.shape[0]
    return jnp.moveaxis(parts, 0, dim).reshape(dims)


def gather_directly(value, axis, dim):
    return joined_along(copy_for_each(value, axis), dim)


def gather_in_order(value, axes, sequence):
    parts = value[None]
    for k in sequence:
        parts = lax.all_gather(parts, axes[k], axis=0, tiled=True)
    block = [lax.axis_size(axes[k]) for k in reversed(sequence)]
    parts = parts.reshape(*block, *value.shape)
    turned = sorted(range(len(sequence)), key=lambda place: sequence[len(sequence) - 1 - place])
    return parts.transpose(*turned, *range(len(sequence), parts.ndim)).reshape(-1, *value.shape)


def gather_axes(value, axes, sequence, dim):
    return joined_along(gather_in_order(value, axes, sequence), dim)


def body(master_gate, master_up, router_weight, router_gain):
    total_gate, total_up = in_one(
        (jnp.sum(master_gate * master_gate, axis=1), jnp.sum(master_up * master_up, axis=1)), "fsdp"
    )
    scale_gate = jnp.sqrt(total_gate)
    scale_up = jnp.sqrt(total_up)
    narrow_gate, narrow_up = (
        (master_gate / jnp.expand_dims(scale_gate, 1)).astype(jnp.bfloat16),
        (master_up / jnp.expand_dims(scale_up, 1)).astype(jnp.bfloat16),
    )
    final_gate, final_up = sent_together((narrow_gate, narrow_up), "fsdp", 0, 1, 2)
    scale_gate = lax.dynamic_slice_in_dim(
        scale_gate, lax.axis_index("fsdp") * final_gate.shape[0], final_gate.shape[0], axis=0
    )
    scale_up = lax.dynamic_slice_in_dim(
        scale_up, lax.axis_index("fsdp") * final_up.shape[0], final_up.shape[0], axis=0
    )
    part_router = (router_weight * router_gain[:, None]).astype(jnp.bfloat16)
    row_router = gather_directly(part_router, "fsdp", 0)
    serve_router = gather_axes(row_router, ("ep_0", "ep_1"), (0, 1), 1)
    return (final_gate, final_up, scale_gate, scale_up, serve_router)


def solution(mesh):
    finer = Mesh(mesh.devices.reshape(4, 2, mesh.shape["fsdp"]), ("ep_0", "ep_1", "fsdp"))
    return jax.shard_map(
        body,
        mesh=finer,
        in_specs=(P(EP, "fsdp", None), P(EP, "fsdp", None), P("fsdp", EP), P("fsdp")),
        out_specs=(
            P(EP_FSDP, None, None),
            P(EP_FSDP, None, None),
            P(EP_FSDP, None),
            P(EP_FSDP, None),
            P(),
        ),
        check_vma=False,
    )
```

profile of v0, /device:TPU:0, one launch (start us, length us, event | category | flops | bytes accessed | tf_op | source)
XLA Modules:
  0.0 161.2 jit_solution(398515752994868322)
XLA Ops:
  0.6 3.3 %multiply_reduce_fusion.1 = f32[16,768]{1,0:T(8,128)S(1)} fusion(f32[16,128,768]{2,1,0:T(8,128)} %param.4), kind=kLoop, calls=%fused_computation.4 | loop fusion | flops 3133440 | bytes 6340608 | tf_op jit(solution)/shard_map/reduce_sum | solution.py:71
  4.0 0.0 copy-start
  4.0 0.0 copy-start.1
  4.0 3.3 %multiply_reduce_fusion = f32[16,768]{1,0:T(8,128)S(1)} fusion(f32[16,128,768]{2,1,0:T(8,128)} %param.5), kind=kLoop, calls=%fused_computation.3 | loop fusion | flops 3133440 | bytes 6340608 | tf_op jit(solution)/shard_map/reduce_sum | solution.py:71
  7.4 2.4 %broadcast_in_dim.4 = f32[16,1,24576]{2,1,0:T(1,128)} broadcast(f32[24576]{0:T(1024)S(1)} %pad_maximum_fusion.1), dimensions={2} | broadcast | bytes 1671168 | tf_op jit(solution)/shard_map/broadcast_in_dim | solution.py:14
  9.7 8.2 %all-to-all-start = ((f32[16,1,24576]{2,1,0:T(1,128)}), f32[16,1,24576]{2,1,0:T(1,128)S(1)}, u32[]{:S(2)}, u32[]{:S(2)}) async-start(f32[16,1,24576]{2,1,0:T(1,128)} %broadcast_in_dim.4), calls=%async_computation | async-start | bytes 3145728 | tf_op jit(solution)/shard_map/all_to_all | solution.py:13
  17.9 0.0 copy-done
  17.9 0.0 copy-done.1
  17.9 24.5 %all-to-all-done = f32[16,1,24576]{2,1,0:T(1,128)S(1)} async-done(((f32[16,1,24576]{2,1,0:T(1,128)}), f32[16,1,24576]{2,1,0:T(1,128)S(1)}, u32[]{:S(2)}, u32[]{:S(2)}) %all-to-all-start) | async-done | bytes 1572896 | tf_op jit(solution)/shard_map/all_to_all | solution.py:13
  42.4 0.6 broadcast_in_dim.5
  43.1 3.5 %all-to-all-start.2 = ((bf16[16,128,16]{1,2,0:T(8,128)(2,1)}), bf16[16,128,16]{1,2,0:T(8,128)(2,1)S(1)}, u32[]{:S(2)}, u32[]{:S(2)}) async-start(bf16[16,128,16]{1,2,0:T(8,128)(2,1)} %broadcast_in_dim.5), calls=%async_computation.2 | async-start | bytes 131072 | tf_op jit(solution)/shard_map/all_to_all | solution.py:13
  46.6 1.0 reduce_sum.29
  47.7 5.3 %divide_convert_fusion = (bf16[16,128,768]{2,1,0:T(8,128)(2,1)S(1)}, bf16[16,128,768]{2,1,0:T(8,128)(2,1)S(1)}) fusion(f32[16,128,768]{2,1,0:T(8,128)} %param.5, f32[16,768]{1,0:T(8,128)S(1)} %sqrt.15, f32[16,128,768]{2,1,0:T(8,128)} %param.4, f32[16,768]{1,0:T(8,128)S(1)} %sqrt.13), kind=kLoop, calls=%fused_computation.1 | loop fusion | flops 6291456 | bytes 18972672 | tf_op jit(solution)/shard_map/convert_element_type | solution.py:77
  53.0 3.2 %pad_maximum_fusion = bf16[16,128,1536]{2,1,0:T(8,128)(2,1)} fusion(bf16[16,128,768]{2,1,0:T(8,128)(2,1)S(1)} %get-tuple-element.39, bf16[16,128,768]{2,1,0:T(8,128)(2,1)S(1)} %get-tuple-element.40), kind=kLoop, calls=%fused_computation | loop fusion | flops 12582912 | bytes 12582912 | tf_op jit(solution)/shard_map/concatenate | solution.py:35
  56.2 0.0 all-to-all-done.2
  56.2 7.2 %all-to-all-start.1 = ((bf16[16,128,1536]{2,1,0:T(8,128)(2,1)}), bf16[16,128,1536]{2,1,0:T(8,128)(2,1)}, u32[]{:S(2)}, u32[]{:S(2)}) async-start(bf16[16,128,1536]{2,1,0:T(8,128)(2,1)} %pad_maximum_fusion), calls=%async_computation.1 | async-start | bytes 12582912 | tf_op jit(solution)/shard_map/all_to_all | solution.py:38
  63.5 12.7 %all_gather.6 = bf16[4,2048,16]{1,2,0:T(8,128)(2,1)S(1)} all-gather(bf16[1,2048,16]{1,2,0:T(8,128)(2,1)S(1)} %broadcast_in_dim_reshape.3), channel_id=1, replica_groups=mesh['ep_0'=4,'ep_1'=2,'fsdp'=16] {'ep_0'}, dimensions={0}, use_global_device_ids=true | all-gather | bytes 327680 | tf_op jit(solution)/shard_map/all_gather | solution.py:58
  76.2 2.2 %all_gather.7 = bf16[8,2048,16]{1,2,0:T(8,128)(2,1)S(1)} all-gather(bf16[4,2048,16]{1,2,0:T(8,128)(2,1)S(1)} %all_gather.6), channel_id=1, replica_groups=mesh['ep_0'=4,'ep_1'=2,'fsdp'=16] {'ep_1'}, dimensions={0}, use_global_device_ids=true | all-gather | bytes 786432 | tf_op jit(solution)/shard_map/all_gather | solution.py:58
  78.4 1.0 copy.24
  79.4 0.6 constant_dynamic-slice_fusion
  80.0 75.3 %all-to-all-done.1 = bf16[16,128,1536]{2,1,0:T(8,128)(2,1)} async-done(((bf16[16,128,1536]{2,1,0:T(8,128)(2,1)}), bf16[16,128,1536]{2,1,0:T(8,128)(2,1)}, u32[]{:S(2)}, u32[]{:S(2)}) %all-to-all-start.1) | async-done | bytes 6291488 | tf_op jit(solution)/shard_map/all_to_all | solution.py:38
  155.2 5.9 %fusion = (bf16[1,2048,768]{2,1,0:T(8,128)(2,1)}, bf16[1,2048,768]{2,1,0:T(8,128)(2,1)}) fusion(bf16[1,2048,1536]{2,1,0:T(8,128)(2,1)} %bitcast), kind=kLoop, calls=%fused_computation.11 | loop fusion | bytes 12582912 | tf_op jit(solution)/shard_map/split | solution.py:37
  (10 shorter events, 0.2 us)
Async XLA Ops:
  4.0 13.9 %copy-start = (f32[128,16]{0,1:T(8,128)S(1)}, f32[128,16]{0,1:T(8,128)}, u32[]{:S(2)}) copy-start(f32[128,16]{0,1:T(8,128)} %param.6) | copy-start | bytes 24580
  4.0 13.9 %copy-start.1 = (f32[128]{0:T(128)S(1)}, f32[128]{0:T(128)}, u32[]{:S(2)}) copy-start(f32[128]{0:T(128)} %param.7) | copy-start | bytes 1540
  9.7 32.7 %all-to-all-start = ((f32[16,1,24576]{2,1,0:T(1,128)}), f32[16,1,24576]{2,1,0:T(1,128)S(1)}, u32[]{:S(2)}, u32[]{:S(2)}) async-start(f32[16,1,24576]{2,1,0:T(1,128)} %broadcast_in_dim.4), calls=%async_computation | async-start | bytes 3145728 | tf_op jit(solution)/shard_map/all_to_all | solution.py:13
  43.1 13.2 %all-to-all-start.2 = ((bf16[16,128,16]{1,2,0:T(8,128)(2,1)}), bf16[16,128,16]{1,2,0:T(8,128)(2,1)S(1)}, u32[]{:S(2)}, u32[]{:S(2)}) async-start(bf16[16,128,16]{1,2,0:T(8,128)(2,1)} %broadcast_in_dim.5), calls=%async_computation.2 | async-start | bytes 131072 | tf_op jit(solution)/shard_map/all_to_all | solution.py:13
  56.2 99.0 %all-to-all-start.1 = ((bf16[16,128,1536]{2,1,0:T(8,128)(2,1)}), bf16[16,128,1536]{2,1,0:T(8,128)(2,1)}, u32[]{:S(2)}, u32[]{:S(2)}) async-start(bf16[16,128,1536]{2,1,0:T(8,128)(2,1)} %pad_maximum_fusion), calls=%async_computation.1 | async-start | bytes 12582912 | tf_op jit(solution)/shard_map/all_to_all | solution.py:38
where the time goes:
time: 162 us; the launch traced here: 161 us
  waiting for transfers between devices  99.7 us (62%)
  starting transfers between devices  18.9 us (12%)
  other arithmetic  16.2 us (10%)
  blocking collectives  14.8 us (9%)
  local copies, waits for them, and re-layouts  10.7 us (7%)
    all_to_all x1, waiting for transfers between devices, sent_together(): lax.all_to_all(both, axis, split_axis=split_dim, concat_axis=concat_dim,...  75.3 us
    all_to_all x2, waiting for transfers between devices, copy_for_each(): lax.all_to_all(jnp.broadcast_to(value[None], (devices, *value.shape)), ax...  24.5 us
    all_gather x2, blocking collectives, gather_in_order(): parts = lax.all_gather(parts, axes[k], axis=0, tiled=True)  14.8 us
    all_to_all x2, starting transfers between devices, copy_for_each(): lax.all_to_all(jnp.broadcast_to(value[None], (devices, *value.shape)), ax...  11.7 us
    all_to_all x1, starting transfers between devices, sent_together(): lax.all_to_all(both, axis, split_axis=split_dim, concat_axis=concat_dim,...  7.2 us
    split x1, local copies, waits for them, and re-layouts, sent_together(): jnp.split(lax.all_to_all(both, axis, split_axis=split_dim, concat_axis=co...  5.95 us
    convert_element_type x1, other arithmetic, body(): (master_up / jnp.expand_dims(scale_up, 1)).astype(jnp.bfloat16)  5.31 us
    reduce_sum x1, other arithmetic, body(): jnp.sum(master_gate * master_gate, axis=1)  3.33 us
  transfers between devices with their start and end apart: 3, of which 2 were waited for; matrix products, arithmetic and copies ran while one was open for 7% of the time, Pallas kernels for 0%

commit v1 on v0

v1 whole, which is shorter than its diff:
```python
import functools

import jax
import jax.numpy as jnp
from jax import lax
from jax.experimental import pallas as pl
from jax.experimental.pallas import tpu as pltpu
from jax.sharding import PartitionSpec as P

MESH = pl.DeviceIdType.MESH
LANES = 128
ORDER = (
    (2, 2), (2, 1), (1, 2), (2, 3), (3, 2), (1, 1), (3, 3), (1, 3),
    (3, 1), (2, 0), (0, 2), (1, 0), (0, 1), (3, 0), (0, 3),
)


def kernel(
    ep_size, side, gate, up, weight, gain,
    final_gate, final_up, scale_gate, scale_up, router,
    x, sums, first, firsts, parts, totals, inverse, sent, rows, columns,
    in_sem, small_sem, first_sem, part_sem, total_sem, row_sem, column_sem, block_sem, own_sem,
):
    fsdp = side * side
    experts, depth = gate.shape[0], gate.shape[1]
    groups = gate.shape[2] // LANES
    chunks = 2 * groups
    ep, me = lax.axis_index("ep"), lax.axis_index("fsdp")
    my_z, my_y = me // side, me % side
    order = [((my_z + dz) % side) * side + (my_y + dy) % side for dy, dz in ORDER]
    others = [(ep + step) % ep_size for step in range(1, ep_size)]

    barrier = pltpu.get_barrier_semaphore()
    for peer in order:
        pl.semaphore_signal(barrier, inc=1, device_id=(ep, peer), device_id_type=MESH)
    for other in others:
        pl.semaphore_signal(barrier, inc=1, device_id=(other, me), device_id_type=MESH)

    def read(chunk):
        source = gate if chunk < groups else up
        at = (chunk % groups) * LANES
        return pltpu.make_async_copy(
            source.at[:, :, pl.ds(at, LANES)], x.at[chunk], in_sem.at[chunk]
        )

    for chunk in range(chunks):
        read(chunk).start()

    def remote(source, target, sems, device):
        return pltpu.make_async_remote_copy(
            src_ref=source, dst_ref=target, send_sem=sems.at[0], recv_sem=sems.at[1],
            device_id=device, device_id_type=MESH,
        )

    def square_sum(chunk, e):
        block = x[chunk, e]
        return jnp.sum(block * block, axis=0, keepdims=True)

    rows[me] = (weight[...] * gain[...]).astype(jnp.bfloat16)

    read(0).wait()
    for e in range(experts):
        total = square_sum(0, e)
        first[pl.ds(e, 1), :] = total
        sums[e, pl.ds(0, 1), :] = total
    pl.semaphore_wait(barrier, len(order) + len(others))
    for peer in order:
        remote(first, firsts.at[me], first_sem, (ep, peer)).start()
    for peer in order:
        remote(rows.at[me], rows.at[me], row_sem, (ep, peer)).start()
    firsts[me] = first[...]

    for chunk in range(1, chunks):
        read(chunk).wait()

    def sum_chunk(chunk, carry):
        for e in range(experts):
            sums[e, pl.ds(chunk, 1), :] = square_sum(chunk, e)
        return carry

    lax.fori_loop(1, chunks, sum_chunk, 0)
    for peer in order:
        remote(sums.at[peer], parts.at[me], part_sem, (ep, peer)).start()
    parts[me] = sums[me]

    def all_of(ref, sem):
        pltpu.make_async_copy(ref, ref, sem).wait()

    def send_chunk(target, chunk, at, scaled):
        columns_at = pl.ds(at, LANES)
        waiting = None
        for peer in order + [me]:
            block = x[chunk, peer] * scaled(peer)
            sent[chunk, peer] = block.astype(jnp.bfloat16)
            if waiting is not None:
                remote(
                    sent.at[chunk, waiting], target.at[pl.ds(me * depth, depth), columns_at],
                    block_sem, (ep, waiting),
                ).start()
            waiting = peer
        pltpu.make_async_copy(
            sent.at[chunk, me], target.at[pl.ds(me * depth, depth), columns_at], own_sem
        ).start()

    all_of(firsts.at[pl.ds(0, fsdp - 1)], first_sem.at[1])
    total = firsts[0]
    for s in range(1, fsdp):
        total = total + firsts[s]
    first_inverse = 1.0 / jnp.sqrt(total)
    for e in range(experts):
        inverse[e, pl.ds(0, 1), :] = first_inverse[e : e + 1, :]
    send_chunk(final_gate, 0, 0, lambda e: inverse[e, pl.ds(0, 1), :])

    all_of(parts.at[pl.ds(0, fsdp - 1)], part_sem.at[1])
    total = parts[0]
    for s in range(1, fsdp):
        total = total + parts[s]
    totals[me] = total
    scale = jnp.sqrt(total)
    for j in range(groups):
        scale_gate[:, j * LANES : (j + 1) * LANES] = scale[j : j + 1, :]
        scale_up[:, j * LANES : (j + 1) * LANES] = scale[groups + j : groups + j + 1, :]
    for peer in order:
        remote(totals.at[me], totals.at[me], total_sem, (ep, peer)).start()

    all_of(rows.at[pl.ds(0, fsdp - 1)], row_sem.at[1])
    for other in others:
        remote(rows, columns.at[ep], column_sem, (other, me)).start()
    pltpu.make_async_copy(rows, columns.at[ep], small_sem).start()

    all_of(totals.at[pl.ds(0, fsdp - 1)], total_sem.at[1])

    def invert(e, carry):
        inverse[e] = 1.0 / jnp.sqrt(totals[e])
        return carry

    lax.fori_loop(0, experts, invert, 0)

    for half, target in enumerate((final_gate, final_up)):

        def send(j, carry, half=half, target=target):
            chunk = half * groups + j
            send_chunk(
                target, chunk, pl.multiple_of(j * LANES, LANES),
                lambda e: inverse[e, pl.ds(chunk, 1), :],
            )
            return carry

        lax.fori_loop(1 - half, groups, send, 0)

    pltpu.make_async_copy(rows, columns.at[ep], small_sem).wait()
    if others:
        all_of(columns.at[pl.ds(0, ep_size - 1)], column_sem.at[1])

    def turn(f, carry):
        block = columns[:, f].astype(jnp.float32).reshape(-1, depth)
        router[pl.ds(pl.multiple_of(f * depth, depth), depth), :] = block.T.astype(jnp.bfloat16)
        return carry

    lax.fori_loop(0, fsdp, turn, 0)

    all_of(firsts.at[pl.ds(0, fsdp - 1)], first_sem.at[0])
    all_of(parts.at[pl.ds(0, fsdp - 1)], part_sem.at[0])
    all_of(totals.at[pl.ds(0, fsdp - 1)], total_sem.at[0])
    all_of(rows.at[pl.ds(0, fsdp - 1)], row_sem.at[0])
    if others:
        all_of(columns.at[pl.ds(0, ep_size - 1)], column_sem.at[0])
    all_of(sent.at[:, 0], own_sem)
    all_of(sent.at[:, pl.ds(0, fsdp - 1)], block_sem.at[0])
    all_of(sent.at[:, pl.ds(0, fsdp - 1)], block_sem.at[1])


def body(ep_size, fsdp, master_gate, master_up, router_weight, router_gain):
    experts, depth, width = master_gate.shape
    side = 4
    own, columns = router_weight.shape[1], 2 * width // LANES
    anywhere = pl.BlockSpec(memory_space=pl.ANY)
    vmem = pl.BlockSpec(memory_space=pltpu.VMEM)
    dma, pair = pltpu.SemaphoreType.DMA, pltpu.SemaphoreType.DMA((2,))
    gate, up, scale_gate, scale_up, router = pl.pallas_call(
        functools.partial(kernel, ep_size, side),
        out_shape=(
            pltpu.VMEM((fsdp * depth, width), jnp.bfloat16),
            pltpu.VMEM((fsdp * depth, width), jnp.bfloat16),
            pltpu.VMEM((1, width), jnp.float32),
            pltpu.VMEM((1, width), jnp.float32),
            pltpu.VMEM((fsdp * depth, ep_size * own), jnp.bfloat16),
        ),
        in_specs=[anywhere, anywhere, vmem, vmem],
        out_specs=[vmem] * 5,
        scratch_shapes=[
            pltpu.VMEM((columns, experts, depth, LANES), jnp.float32),
            pltpu.VMEM((experts, columns, LANES), jnp.float32),
            pltpu.VMEM((experts, LANES), jnp.float32),
            pltpu.VMEM((fsdp, experts, LANES), jnp.float32),
            pltpu.VMEM((fsdp, columns, LANES), jnp.float32),
            pltpu.VMEM((fsdp, columns, LANES), jnp.float32),
            pltpu.VMEM((experts, columns, LANES), jnp.float32),
            pltpu.VMEM((columns, experts, depth, LANES), jnp.bfloat16),
            pltpu.VMEM((fsdp, own, depth), jnp.bfloat16),
            pltpu.VMEM((ep_size, fsdp, own, depth), jnp.bfloat16),
            dma((columns,)), dma,
            pair, pair, pair, pair, pair, pair, dma,
        ],
        compiler_params=pltpu.CompilerParams(
            collective_id=0, has_side_effects=True, vmem_limit_bytes=48 * 2**20
        ),
        name="relayout",
    )(master_gate, master_up, router_weight.T, router_gain[None, :])
    return gate[None], up[None], scale_gate, scale_up, router


def solution(mesh):
    both = ("ep", "fsdp")
    return jax.shard_map(
        functools.partial(body, mesh.shape["ep"], mesh.shape["fsdp"]),
        mesh=mesh,
        in_specs=(P("ep", "fsdp", None), P("ep", "fsdp", None), P("fsdp", "ep"), P("fsdp")),
        out_specs=(P(both, None, None), P(both, None, None), P(both, None), P(both, None), P()),
        check_vma=False,
    )
```

time: 162 us -> 91.6 us (0.57)
  waiting for transfers between devices: 99.7 us -> 0 us
  Pallas kernels: 0 us -> 85.5 us
  starting transfers between devices: 18.9 us -> 0 us
  other arithmetic: 16.2 us -> 0 us
  blocking collectives: 14.8 us -> 0 us
  local copies, waits for them, and re-layouts: 10.7 us -> 5.28 us
    all_to_all x3 -> x0, waiting for transfers between devices: 99.7 us -> none  [the longest x1 75.3 us: sent_together(): lax.all_to_all(both, axis, split_axis=split_dim, concat_axis=concat_dim,...]
    pallas_call x0 -> x1, Pallas kernels: none -> 85.5 us  [body(): pl.pallas_call(functools.partial(kernel, ep_size, side), out_shape=(pltpu...]
    all_to_all x3 -> x0, starting transfers between devices: 18.9 us -> none  [the longest x2 11.7 us: copy_for_each(): lax.all_to_all(jnp.broadcast_to(value[None], (devices, *value.shape)), ax...]
    all_gather x2 -> x0, blocking collectives: 14.8 us -> none  [gather_in_order(): parts = lax.all_gather(parts, axes[k], axis=0, tiled=True)]
    reduce_sum x3 -> x0, other arithmetic: 7.69 us -> none  [the longest x1 3.33 us: body(): jnp.sum(master_gate * master_gate, axis=1)]
    split x1 -> x0, local copies, waits for them, and re-layouts: 5.95 us -> none  [sent_together(): jnp.split(lax.all_to_all(both, axis, split_axis=split_dim, concat_axis=co...]
    convert_element_type x2 -> x0, other arithmetic: 5.31 us -> none  [the longest x1 5.31 us: body(): (master_up / jnp.expand_dims(scale_up, 1)).astype(jnp.bfloat16)]
    unnamed x5, local copies, waits for them, and re-layouts: 1.01 us -> 5.28 us
  transfers between devices with their start and end apart: 3 -> 0, of which waited for: 2 -> 0; matrix products, arithmetic and copies ran while one was open for 7% -> 0% of each run, Pallas kernels for 0% -> 0%
where the time goes in v1:
time: 91.6 us; the launch traced here: 91.4 us
  Pallas kernels  85.5 us (93%)
  local copies, waits for them, and re-layouts  5.28 us (6%)
    pallas_call x1, Pallas kernels, body(): pl.pallas_call(functools.partial(kernel, ep_size, side), out_shape=(pltpu...  85.5 us
    unnamed x5, local copies, waits for them, and re-layouts  5.28 us

profile of v1, /device:TPU:0, one launch (start us, length us, event | category | flops | bytes accessed | tf_op | source)
XLA Modules:
  0.0 91.4 jit_solution(10118149882238974628)
XLA Ops:
  0.6 85.5 %relayout.1 = (bf16[2048,768]{1,0:T(8,128)(2,1)S(1)}, bf16[2048,768]{1,0:T(8,128)(2,1)S(1)}, f32[1,768]{1,0:T(1,128)S(1)}, f32[1,768]{1,0:T(1,128)S(1)}, bf16[2048,128]{1,0:T(8,128)(2,1)S(1)}) custom-call(f32[16,128,768]{2,1,0:T(8,128)} %gate.1, f32[16,128,768]{2,1,0:T(8,128)} %up.1, f32[16,128]{1,0:T(8,128)} %bitcast.6, f32[1,128]{1,0:T(1,128)} %bitcast.7), custom_call_target="tpu_custom_call" | custom-call | tf_op jit(solution)/shard_map/relayout/pallas_call | solution.py:180
  86.2 1.7 %copy.14 = bf16[1,2048,768]{2,1,0:T(8,128)(2,1)} copy(bf16[1,2048,768]{2,1,0:T(8,128)(2,1)S(1)} %bitcast.5) | data formatting | bytes 6291456
  87.8 1.7 %copy.15 = bf16[1,2048,768]{2,1,0:T(8,128)(2,1)} copy(bf16[1,2048,768]{2,1,0:T(8,128)(2,1)S(1)} %bitcast.4) | data formatting | bytes 6291456
  89.5 0.6 copy.16
  90.1 0.6 copy.17
  90.6 0.8 copy.18

commit v2 on v1

v2 whole, which is shorter than its diff:
```python
import functools

import jax
import jax.numpy as jnp
from jax import lax
from jax.experimental import pallas as pl
from jax.experimental.pallas import tpu as pltpu
from jax.sharding import PartitionSpec as P

MESH = pl.DeviceIdType.MESH
LANES = 128
HEAD = 5
ORDER = (
    (2, 2), (2, 1), (1, 2), (2, 3), (3, 2), (1, 1), (3, 3), (1, 3),
    (3, 1), (2, 0), (0, 2), (1, 0), (0, 1), (3, 0), (0, 3),
)


def kernel(
    ep_size, side, stages, gate, up, weight, gain,
    final_gate, final_up, scale_gate, scale_up, router,
    x, sums, parts, totals, inverse, sent, rows, columns,
    in_sem, small_sem, part_sem, total_sem, row_sem, column_sem, block_sem, own_sem,
):
    fsdp = side * side
    experts, depth = gate.shape[0], gate.shape[1]
    groups = gate.shape[2] // LANES
    chunks = 2 * groups
    ep, me = lax.axis_index("ep"), lax.axis_index("fsdp")
    my_z, my_y = me // side, me % side
    order = [((my_z + dz) % side) * side + (my_y + dy) % side for dy, dz in ORDER]
    others = [(ep + step) % ep_size for step in range(1, ep_size)]
    scales = (scale_gate, scale_up)

    barrier = pltpu.get_barrier_semaphore()
    for peer in order:
        pl.semaphore_signal(barrier, inc=1, device_id=(ep, peer), device_id_type=MESH)
    for other in others:
        pl.semaphore_signal(barrier, inc=1, device_id=(other, me), device_id_type=MESH)

    def read(chunk):
        source = gate if chunk < groups else up
        at = (chunk % groups) * LANES
        return pltpu.make_async_copy(
            source.at[:, :, pl.ds(at, LANES)], x.at[chunk], in_sem.at[chunk]
        )

    for chunk in range(chunks):
        read(chunk).start()

    def remote(source, target, sems, device):
        return pltpu.make_async_remote_copy(
            src_ref=source, dst_ref=target, send_sem=sems.at[0], recv_sem=sems.at[1],
            device_id=device, device_id_type=MESH,
        )

    def all_of(ref, sem):
        pltpu.make_async_copy(ref, ref, sem).wait()

    def square_sum(chunk, e):
        block = x[chunk, e]
        return jnp.sum(block * block, axis=0, keepdims=True)

    def take_sums(stage):
        start, stop = stages[stage]
        for chunk in range(start, stop):
            read(chunk).wait()

        def one(chunk, carry):
            for e in range(experts):
                sums[stage][e, pl.ds(chunk - start, 1), :] = square_sum(chunk, e)
            return carry

        lax.fori_loop(start, stop, one, 0)

    def send_sums(stage):
        for peer in order:
            remote(sums[stage].at[peer], parts[stage].at[me], part_sem.at[stage], (ep, peer)).start()
        parts[stage][me] = sums[stage][me]

    def send_totals(stage):
        start, stop = stages[stage]
        all_of(parts[stage].at[pl.ds(0, fsdp - 1)], part_sem.at[stage, 1])
        total = parts[stage][0]
        for s in range(1, fsdp):
            total = total + parts[stage][s]
        totals[stage][me] = total
        scale = jnp.sqrt(total)
        for peer in order:
            remote(totals[stage].at[me], totals[stage].at[me], total_sem.at[stage], (ep, peer)).start()
        for chunk in range(start, stop):
            at = (chunk % groups) * LANES
            scales[chunk // groups][:, at : at + LANES] = scale[chunk - start : chunk - start + 1, :]

    def take_totals(stage):
        all_of(totals[stage].at[pl.ds(0, fsdp - 1)], total_sem.at[stage, 1])

        def invert(e, carry):
            inverse[stage][e] = 1.0 / jnp.sqrt(totals[stage][e])
            return carry

        lax.fori_loop(0, experts, invert, 0)

    def send_blocks(target, chunk, at, peers, scaled):
        place = (pl.ds(me * depth, depth), pl.ds(at, LANES))
        waiting = None
        for peer in peers + [None]:
            if peer is not None:
                sent[chunk, peer] = (x[chunk, peer] * scaled(peer)).astype(jnp.bfloat16)
            if waiting is not None:
                remote(sent.at[chunk, waiting], target.at[place], block_sem, (ep, waiting)).start()
            waiting = peer

    def keep_block(target, chunk, at, scaled):
        sent[chunk, me] = (x[chunk, me] * scaled(me)).astype(jnp.bfloat16)
        place = (pl.ds(me * depth, depth), pl.ds(at, LANES))
        pltpu.make_async_copy(sent.at[chunk, me], target.at[place], own_sem).start()

    def send_stage(stage):
        for half, target in enumerate((final_gate, final_up)):
            start = max(stages[stage][0], half * groups)
            stop = min(stages[stage][1], half * groups + groups)

            def send(chunk, carry, half=half, target=target):
                at = pl.multiple_of((chunk - half * groups) * LANES, LANES)
                scaled = lambda e: inverse[stage][e, pl.ds(chunk - stages[stage][0], 1), :]
                send_blocks(target, chunk, at, order, scaled)
                keep_block(target, chunk, at, scaled)
                return carry

            if start < stop:
                lax.fori_loop(start, stop, send, 0)

    rows[me] = (weight[...] * gain[...]).astype(jnp.bfloat16)

    read(0).wait()
    for e in range(experts):
        sums[0][pl.ds(e, 1), :] = square_sum(0, e)
    pl.semaphore_wait(barrier, len(order) + len(others))
    for peer in order:
        remote(sums[0], parts[0].at[me], part_sem.at[0], (ep, peer)).start()
    for peer in order:
        remote(rows.at[me], rows.at[me], row_sem, (ep, peer)).start()
    parts[0][me] = sums[0][...]

    for stage in range(1, len(stages)):
        take_sums(stage)
        send_sums(stage)

    all_of(parts[0].at[pl.ds(0, fsdp - 1)], part_sem.at[0, 1])
    total = parts[0][0]
    for s in range(1, fsdp):
        total = total + parts[0][s]
    totals[0][...] = total
    inverse[0][...] = 1.0 / jnp.sqrt(total)
    scale_gate[:, :LANES] = jnp.sqrt(totals[0][pl.ds(me, 1), :])
    scaled = lambda e: inverse[0][pl.ds(e, 1), :]

    send_blocks(final_gate, 0, 0, order[:HEAD], scaled)
    send_totals(1)
    send_blocks(final_gate, 0, 0, order[HEAD:], scaled)
    keep_block(final_gate, 0, 0, scaled)
    for stage in range(2, len(stages)):
        send_totals(stage)

    all_of(rows.at[pl.ds(0, fsdp - 1)], row_sem.at[1])
    for other in others:
        remote(rows, columns.at[ep], column_sem, (other, me)).start()
    pltpu.make_async_copy(rows, columns.at[ep], small_sem).start()

    for stage in range(1, len(stages)):
        take_totals(stage)
        send_stage(stage)

    pltpu.make_async_copy(rows, columns.at[ep], small_sem).wait()
    if others:
        all_of(columns.at[pl.ds(0, ep_size - 1)], column_sem.at[1])

    def turn(f, carry):
        block = columns[:, f].astype(jnp.float32).reshape(-1, depth)
        router[pl.ds(pl.multiple_of(f * depth, depth), depth), :] = block.T.astype(jnp.bfloat16)
        return carry

    lax.fori_loop(0, fsdp, turn, 0)

    for stage in range(len(stages)):
        all_of(parts[stage].at[pl.ds(0, fsdp - 1)], part_sem.at[stage, 0])
        if stage > 0:
            all_of(totals[stage].at[pl.ds(0, fsdp - 1)], total_sem.at[stage, 0])
    all_of(rows.at[pl.ds(0, fsdp - 1)], row_sem.at[0])
    if others:
        all_of(columns.at[pl.ds(0, ep_size - 1)], column_sem.at[0])
    all_of(sent.at[:, 0], own_sem)
    all_of(sent.at[:, pl.ds(0, fsdp - 1)], block_sem.at[0])
    all_of(sent.at[:, pl.ds(0, fsdp - 1)], block_sem.at[1])


def place(*refs):
    count = (len(refs) - 1) // 2
    copies = []
    for source, target in zip(refs[:count], refs[count : 2 * count]):
        pieces = 4 if source.shape[0] > 8 else 1
        step = source.shape[0] // pieces
        for k in range(pieces):
            at = pl.ds(k * step, step)
            copies.append(pltpu.make_async_copy(source.at[at], target.at[at], refs[-1].at[len(copies)]))
    for copy in copies:
        copy.start()
    for copy in copies:
        copy.wait()


def body(ep_size, fsdp, master_gate, master_up, router_weight, router_gain):
    experts, depth, width = master_gate.shape
    side = 4
    own, chunks = router_weight.shape[1], 2 * width // LANES
    stages = ((0, 1), (1, 4), (4, chunks))
    anywhere = pl.BlockSpec(memory_space=pl.ANY)
    vmem = pl.BlockSpec(memory_space=pltpu.VMEM)
    dma, pair = pltpu.SemaphoreType.DMA, pltpu.SemaphoreType.DMA((2,))

    def per_stage(lead, dtype=jnp.float32):
        return [pltpu.VMEM((lead, stop - start, LANES), dtype) for start, stop in stages[1:]]

    results = (
        ((fsdp * depth, width), jnp.bfloat16),
        ((fsdp * depth, width), jnp.bfloat16),
        ((1, width), jnp.float32),
        ((1, width), jnp.float32),
        ((fsdp * depth, ep_size * own), jnp.bfloat16),
    )
    flat = pltpu.VMEM((experts, LANES), jnp.float32)
    arrived = pl.pallas_call(
        functools.partial(kernel, ep_size, side, stages),
        out_shape=tuple(pltpu.VMEM(*result) for result in results),
        in_specs=[anywhere, anywhere, vmem, vmem],
        out_specs=[vmem] * 5,
        scratch_shapes=[
            pltpu.VMEM((chunks, experts, depth, LANES), jnp.float32),
            [flat] + per_stage(experts),
            [pltpu.VMEM((fsdp, experts, LANES), jnp.float32)] + per_stage(fsdp),
            [flat] + per_stage(experts),
            [flat] + per_stage(experts),
            pltpu.VMEM((chunks, experts, depth, LANES), jnp.bfloat16),
            pltpu.VMEM((fsdp, own, depth), jnp.bfloat16),
            pltpu.VMEM((ep_size, fsdp, own, depth), jnp.bfloat16),
            dma((chunks,)), dma, dma((len(stages), 2)), dma((len(stages), 2)),
            pair, pair, pair, dma,
        ],
        compiler_params=pltpu.CompilerParams(
            collective_id=0, has_side_effects=True, vmem_limit_bytes=48 * 2**20
        ),
        name="relayout",
    )(master_gate, master_up, router_weight.T, router_gain[None, :])
    gate, up, scale_gate, scale_up, router = pl.pallas_call(
        place,
        out_shape=tuple(jax.ShapeDtypeStruct(*result) for result in results),
        in_specs=[vmem] * 5,
        out_specs=[anywhere] * 5,
        scratch_shapes=[dma((16,))],
        compiler_params=pltpu.CompilerParams(vmem_limit_bytes=2**20),
        name="place",
    )(*(pltpu.with_memory_space_constraint(a, pltpu.VMEM) for a in arrived))
    return gate[None], up[None], scale_gate, scale_up, router


def solution(mesh):
    both = ("ep", "fsdp")
    return jax.shard_map(
        functools.partial(body, mesh.shape["ep"], mesh.shape["fsdp"]),
        mesh=mesh,
        in_specs=(P("ep", "fsdp", None), P("ep", "fsdp", None), P("fsdp", "ep"), P("fsdp")),
        out_specs=(P(both, None, None), P(both, None, None), P(both, None), P(both, None), P()),
        check_vma=False,
    )
```

time: 91.6 us -> 88.1 us (0.962)
  local copies, waits for them, and re-layouts: 5.28 us -> 0 us
    unnamed x5 -> x0, local copies, waits for them, and re-layouts: 5.28 us -> none
    pallas_call x1 -> x2, Pallas kernels: 85.5 us -> 86.4 us  [the longest x1 83.5 us: body(): pl.pallas_call(functools.partial(kernel, ep_size, side, stages), out_shap...]
where the time goes in v2:
time: 88.1 us; the launch traced here: 87 us
  Pallas kernels  86.4 us (98%)
    pallas_call x1, Pallas kernels, body(): pl.pallas_call(functools.partial(kernel, ep_size, side, stages), out_shap...  83.5 us
    pallas_call x1, Pallas kernels, body(): pl.pallas_call(place, out_shape=tuple((jax.ShapeDtypeStruct(*result) for...  2.95 us

profile of v2, /device:TPU:0, one launch (start us, length us, event | category | flops | bytes accessed | tf_op | source)
XLA Modules:
  0.0 87.0 jit_solution(3819404697266712882)
XLA Ops:
  0.6 83.5 %relayout.1 = (bf16[2048,768]{1,0:T(8,128)(2,1)S(1)}, bf16[2048,768]{1,0:T(8,128)(2,1)S(1)}, f32[1,768]{1,0:T(1,128)S(1)}, f32[1,768]{1,0:T(1,128)S(1)}, bf16[2048,128]{1,0:T(8,128)(2,1)S(1)}) custom-call(f32[16,128,768]{2,1,0:T(8,128)} %gate.1, f32[16,128,768]{2,1,0:T(8,128)} %up.1, f32[16,128]{1,0:T(8,128)} %bitcast.4, f32[1,128]{1,0:T(1,128)} %bitcast.5), custom_call_target="tpu_custom_call" | custom-call | tf_op jit(solution)/shard_map/relayout/pallas_call | solution.py:233
  84.1 3.0 %place.1 = (bf16[2048,768]{1,0:T(8,128)(2,1)}, bf16[2048,768]{1,0:T(8,128)(2,1)}, f32[1,768]{1,0:T(1,128)}, f32[1,768]{1,0:T(1,128)}, bf16[2048,128]{1,0:T(8,128)(2,1)}) custom-call(bf16[2048,768]{1,0:T(8,128)(2,1)S(1)} %get-tuple-element.15.refs_0_, bf16[2048,768]{1,0:T(8,128)(2,1)S(1)} %get-tuple-element.16.refs_1_, ...), custom_call_target="tpu_custom_call" | custom-call | tf_op jit(solution)/shard_map/place/pallas_call | solution.py:255

commit v3 on v2

--- a/solution.py
+++ b/solution.py
@@ -9,7 +9,9 @@
 
 MESH = pl.DeviceIdType.MESH
 LANES = 128
-HEAD = 5
+HEAD = 0
+RAW = 16
+PIECE = 4
 ORDER = (
     (2, 2), (2, 1), (1, 2), (2, 3), (3, 2), (1, 1), (3, 3), (1, 3),
     (3, 1), (2, 0), (0, 2), (1, 0), (0, 1), (3, 0), (0, 3),
@@ -19,8 +21,8 @@
 def kernel(
     ep_size, side, stages, gate, up, weight, gain,
     final_gate, final_up, scale_gate, scale_up, router,
-    x, sums, parts, totals, inverse, sent, rows, columns,
-    in_sem, small_sem, part_sem, total_sem, row_sem, column_sem, block_sem, own_sem,
+    x, sums, parts, totals, inverse, sent, raw, mine, rows, columns,
+    in_sem, small_sem, part_sem, total_sem, raw_sem, row_sem, column_sem, block_sem, last_sem, own_sem, ready_sem,
 ):
     fsdp = side * side
     experts, depth = gate.shape[0], gate.shape[1]
@@ -31,22 +33,40 @@
     order = [((my_z + dz) % side) * side + (my_y + dy) % side for dy, dz in ORDER]
     others = [(ep + step) % ep_size for step in range(1, ep_size)]
     scales = (scale_gate, scale_up)
+    last, short = (groups - 1) * LANES, depth - RAW
 
     barrier = pltpu.get_barrier_semaphore()
+    reads = []
+    for half, source in enumerate((gate, up)):
+        for start, stop in ((0, 1), (1, 4), (4, groups)) if half == 0 else ((0, groups),):
+            for e in range(0, experts, PIECE):
+                part = (pl.ds(e, PIECE), slice(None), pl.ds(start * LANES, (stop - start) * LANES))
+                copy = pltpu.make_async_copy(
+                    source.at[part], x.at[(half, *part)], in_sem.at[len(reads)]
+                )
+                reads.append((half * groups + start, copy))
+    for chunk, copy in reads:
+        if chunk == 0:
+            copy.start()
     for peer in order:
         pl.semaphore_signal(barrier, inc=1, device_id=(ep, peer), device_id_type=MESH)
     for other in others:
-        pl.semaphore_signal(barrier, inc=1, device_id=(other, me), device_id_type=MESH)
-
-    def read(chunk):
-        source = gate if chunk < groups else up
-        at = (chunk % groups) * LANES
-        return pltpu.make_async_copy(
-            source.at[:, :, pl.ds(at, LANES)], x.at[chunk], in_sem.at[chunk]
-        )
-
-    for chunk in range(chunks):
-        read(chunk).start()
+        @pl.when(other > ep)
+        def _(other=other):
+            pl.semaphore_signal(barrier, inc=1, device_id=(other, me), device_id_type=MESH)
+
+    for chunk, copy in reads:
+        if chunk > 0:
+            copy.start()
+
+    def wait_reads(start, stop):
+        for chunk, copy in reads:
+            if start <= chunk < stop:
+                copy.wait()
+
+    def block_of(chunk, e):
+        half = chunk // groups
+        return x[half, e, :, pl.ds(pl.multiple_of((chunk - half * groups) * LANES, LANES), LANES)]
 
     def remote(source, target, sems, device):
         return pltpu.make_async_remote_copy(
@@ -58,13 +78,12 @@
         pltpu.make_async_copy(ref, ref, sem).wait()
 
     def square_sum(chunk, e):
-        block = x[chunk, e]
+        block = block_of(chunk, e)
         return jnp.sum(block * block, axis=0, keepdims=True)
 
     def take_sums(stage):
         start, stop = stages[stage]
-        for chunk in range(start, stop):
-            read(chunk).wait()
+        wait_reads(start, stop)
 
         def one(chunk, carry):
             for e in range(experts):
@@ -85,6 +104,8 @@
         for s in range(1, fsdp):
             total = total + parts[stage][s]
         totals[stage][me] = total
+        if stop == chunks:
+            mine[...] = 1.0 / jnp.sqrt(total)
         scale = jnp.sqrt(total)
         for peer in order:
             remote(totals[stage].at[me], totals[stage].at[me], total_sem.at[stage], (ep, peer)).start()
@@ -101,18 +122,20 @@
 
         lax.fori_loop(0, experts, invert, 0)
 
-    def send_blocks(target, chunk, at, peers, scaled):
-        place = (pl.ds(me * depth, depth), pl.ds(at, LANES))
+    def send_blocks(target, chunk, at, peers, scaled, height=depth, sems=block_sem):
+        place = (pl.ds(me * depth, height), pl.ds(at, LANES))
         waiting = None
         for peer in peers + [None]:
             if peer is not None:
-                sent[chunk, peer] = (x[chunk, peer] * scaled(peer)).astype(jnp.bfloat16)
+                block = block_of(chunk, peer)[:height] * scaled(peer)
+                sent[chunk, peer, :height] = block.astype(jnp.bfloat16)
             if waiting is not None:
-                remote(sent.at[chunk, waiting], target.at[place], block_sem, (ep, waiting)).start()
+                source = sent.at[chunk, waiting, pl.ds(0, height)]
+                remote(source, target.at[place], sems, (ep, waiting)).start()
             waiting = peer
 
     def keep_block(target, chunk, at, scaled):
-        sent[chunk, me] = (x[chunk, me] * scaled(me)).astype(jnp.bfloat16)
+        sent[chunk, me] = (block_of(chunk, me) * scaled(me)).astype(jnp.bfloat16)
         place = (pl.ds(me * depth, depth), pl.ds(at, LANES))
         pltpu.make_async_copy(sent.at[chunk, me], target.at[place], own_sem).start()
 
@@ -120,6 +143,7 @@
         for half, target in enumerate((final_gate, final_up)):
             start = max(stages[stage][0], half * groups)
             stop = min(stages[stage][1], half * groups + groups)
+            ends = stop == chunks
 
             def send(chunk, carry, half=half, target=target):
                 at = pl.multiple_of((chunk - half * groups) * LANES, LANES)
@@ -129,23 +153,36 @@
                 return carry
 
             if start < stop:
-                lax.fori_loop(start, stop, send, 0)
+                lax.fori_loop(start, stop - ends, send, 0)
+            if ends:
+                scaled = lambda e: inverse[stage][e, pl.ds(chunks - 1 - stages[stage][0], 1), :]
+                send_blocks(target, chunks - 1, last, order, scaled, short, last_sem)
+                keep_block(target, chunks - 1, last, scaled)
 
     rows[me] = (weight[...] * gain[...]).astype(jnp.bfloat16)
 
-    read(0).wait()
+    wait_reads(0, 1)
     for e in range(experts):
         sums[0][pl.ds(e, 1), :] = square_sum(0, e)
-    pl.semaphore_wait(barrier, len(order) + len(others))
+    pl.semaphore_wait(barrier, len(order) + ep)
     for peer in order:
         remote(sums[0], parts[0].at[me], part_sem.at[0], (ep, peer)).start()
-    for peer in order:
-        remote(rows.at[me], rows.at[me], row_sem, (ep, peer)).start()
     parts[0][me] = sums[0][...]
+    for other in others:
+
+        @pl.when(other < ep)
+        def _(other=other):
+            pl.semaphore_signal(ready_sem, inc=1, device_id=(other, me), device_id_type=MESH)
 
     for stage in range(1, len(stages)):
         take_sums(stage)
         send_sums(stage)
+        if stage == 1:
+            for peer in order:
+                remote(rows.at[me], rows.at[me], row_sem, (ep, peer)).start()
+            for peer in order:
+                source = up.at[peer, pl.ds(short, RAW), pl.ds(last, LANES)]
+                remote(source, raw.at[me], raw_sem, (ep, peer)).start()
 
     all_of(parts[0].at[pl.ds(0, fsdp - 1)], part_sem.at[0, 1])
     total = parts[0][0]
@@ -164,6 +201,11 @@
         send_totals(stage)
 
     all_of(rows.at[pl.ds(0, fsdp - 1)], row_sem.at[1])
+
+    @pl.when(ep < ep_size - 1)
+    def _():
+        pl.semaphore_wait(ready_sem, ep_size - 1 - ep)
+
     for other in others:
         remote(rows, columns.at[ep], column_sem, (other, me)).start()
     pltpu.make_async_copy(rows, columns.at[ep], small_sem).start()
@@ -171,6 +213,13 @@
     for stage in range(1, len(stages)):
         take_totals(stage)
         send_stage(stage)
+
+    all_of(raw.at[pl.ds(0, fsdp - 1)], raw_sem.at[1])
+    final = mine[pl.ds(stages[-1][1] - stages[-1][0] - 1, 1), :]
+    for step in range(1, fsdp):
+        source = lax.rem(me + step, fsdp)
+        at = pl.multiple_of(source * depth + short, RAW)
+        final_up[pl.ds(at, RAW), last : last + LANES] = (raw[source] * final).astype(jnp.bfloat16)
 
     pltpu.make_async_copy(rows, columns.at[ep], small_sem).wait()
     if others:
@@ -191,8 +240,10 @@
     if others:
         all_of(columns.at[pl.ds(0, ep_size - 1)], column_sem.at[0])
     all_of(sent.at[:, 0], own_sem)
-    all_of(sent.at[:, pl.ds(0, fsdp - 1)], block_sem.at[0])
-    all_of(sent.at[:, pl.ds(0, fsdp - 1)], block_sem.at[1])
+    all_of(raw.at[pl.ds(0, fsdp - 1)], raw_sem.at[0])
+    for k in range(2):
+        all_of(sent.at[: chunks - 1, pl.ds(0, fsdp - 1)], block_sem.at[k])
+        all_of(sent.at[chunks - 1, pl.ds(0, fsdp - 1), pl.ds(0, short)], last_sem.at[k])
 
 
 def place(*refs):
@@ -236,16 +287,18 @@
         in_specs=[anywhere, anywhere, vmem, vmem],
         out_specs=[vmem] * 5,
         scratch_shapes=[
-            pltpu.VMEM((chunks, experts, depth, LANES), jnp.float32),
+            pltpu.VMEM((2, experts, depth, width), jnp.float32),
             [flat] + per_stage(experts),
             [pltpu.VMEM((fsdp, experts, LANES), jnp.float32)] + per_stage(fsdp),
             [flat] + per_stage(experts),
             [flat] + per_stage(experts),
             pltpu.VMEM((chunks, experts, depth, LANES), jnp.bfloat16),
+            pltpu.VMEM((fsdp, RAW, LANES), jnp.float32),
+            pltpu.VMEM((stages[-1][1] - stages[-1][0], LANES), jnp.float32),
             pltpu.VMEM((fsdp, own, depth), jnp.bfloat16),
             pltpu.VMEM((ep_size, fsdp, own, depth), jnp.bfloat16),
-            dma((chunks,)), dma, dma((len(stages), 2)), dma((len(stages), 2)),
-            pair, pair, pair, dma,
+            dma((4 * experts // PIECE,)), dma, dma((len(stages), 2)), dma((len(stages), 2)),
+            pair, pair, pair, pair, pair, dma, pltpu.SemaphoreType.REGULAR,
         ],
         compiler_params=pltpu.CompilerParams(
             collective_id=0, has_side_effects=True, vmem_limit_bytes=48 * 2**20

time: 88.1 us -> 86.3 us (0.980)
  Pallas kernels: 86.4 us -> 85.5 us
    pallas_call x1, Pallas kernels: 83.5 us -> 82.5 us  [body(): pl.pallas_call(functools.partial(kernel, ep_size, side, stages), out_shap...]
where the time goes in v3:
time: 86.3 us; the launch traced here: 86.1 us
  Pallas kernels  85.5 us (99%)
    pallas_call x1, Pallas kernels, body(): pl.pallas_call(functools.partial(kernel, ep_size, side, stages), out_shap...  82.5 us
    pallas_call x1, Pallas kernels, body(): pl.pallas_call(place, out_shape=tuple((jax.ShapeDtypeStruct(*result) for...  2.95 us

profile of v3, /device:TPU:0, one launch (start us, length us, event | category | flops | bytes accessed | tf_op | source)
XLA Modules:
  0.0 86.1 jit_solution(4939121037279584814)
XLA Ops:
  0.6 82.5 %relayout.1 = (bf16[2048,768]{1,0:T(8,128)(2,1)S(1)}, bf16[2048,768]{1,0:T(8,128)(2,1)S(1)}, f32[1,768]{1,0:T(1,128)S(1)}, f32[1,768]{1,0:T(1,128)S(1)}, bf16[2048,128]{1,0:T(8,128)(2,1)S(1)}) custom-call(f32[16,128,768]{2,1,0:T(8,128)} %gate.1, f32[16,128,768]{2,1,0:T(8,128)} %up.1, f32[16,128]{1,0:T(8,128)} %bitcast.4, f32[1,128]{1,0:T(1,128)} %bitcast.5), custom_call_target="tpu_custom_call" | custom-call | tf_op jit(solution)/shard_map/relayout/pallas_call | solution.py:284
  83.1 3.0 %place.1 = (bf16[2048,768]{1,0:T(8,128)(2,1)}, bf16[2048,768]{1,0:T(8,128)(2,1)}, f32[1,768]{1,0:T(1,128)}, f32[1,768]{1,0:T(1,128)}, bf16[2048,128]{1,0:T(8,128)(2,1)}) custom-call(bf16[2048,768]{1,0:T(8,128)(2,1)S(1)} %get-tuple-element.15.refs_0_, bf16[2048,768]{1,0:T(8,128)(2,1)S(1)} %get-tuple-element.16.refs_1_, ...), custom_call_target="tpu_custom_call" | custom-call | tf_op jit(solution)/shard_map/place/pallas_call | solution.py:308

commit v4 on v3

--- a/solution.py
+++ b/solution.py
@@ -9,7 +9,7 @@
 
 MESH = pl.DeviceIdType.MESH
 LANES = 128
-HEAD = 0
+HEAD = 3
 RAW = 16
 PIECE = 4
 ORDER = (
@@ -21,8 +21,8 @@
 def kernel(
     ep_size, side, stages, gate, up, weight, gain,
     final_gate, final_up, scale_gate, scale_up, router,
-    x, sums, parts, totals, inverse, sent, raw, mine, rows, columns,
-    in_sem, small_sem, part_sem, total_sem, raw_sem, row_sem, column_sem, block_sem, last_sem, own_sem, ready_sem,
+    x, sums, parts, totals, inverse, sent, raw, mine, weight_here, gain_here, rows, columns,
+    in_sem, small_sem, part_sem, total_sem, raw_sem, row_sem, column_sem, block_sem, last_sem, own_sem, ready_sem, weight_sem,
 ):
     fsdp = side * side
     experts, depth = gate.shape[0], gate.shape[1]
@@ -48,6 +48,12 @@
     for chunk, copy in reads:
         if chunk == 0:
             copy.start()
+    small = (
+        pltpu.make_async_copy(weight, weight_here, weight_sem.at[0]),
+        pltpu.make_async_copy(gain, gain_here, weight_sem.at[1]),
+    )
+    for copy in small:
+        copy.start()
     for peer in order:
         pl.semaphore_signal(barrier, inc=1, device_id=(ep, peer), device_id_type=MESH)
     for other in others:
@@ -159,8 +165,6 @@
                 send_blocks(target, chunks - 1, last, order, scaled, short, last_sem)
                 keep_block(target, chunks - 1, last, scaled)
 
-    rows[me] = (weight[...] * gain[...]).astype(jnp.bfloat16)
-
     wait_reads(0, 1)
     for e in range(experts):
         sums[0][pl.ds(e, 1), :] = square_sum(0, e)
@@ -178,6 +182,9 @@
         take_sums(stage)
         send_sums(stage)
         if stage == 1:
+            for copy in small:
+                copy.wait()
+            rows[me] = (weight_here[...] * gain_here[...]).astype(jnp.bfloat16)
             for peer in order:
                 remote(rows.at[me], rows.at[me], row_sem, (ep, peer)).start()
             for peer in order:
@@ -265,7 +272,7 @@
     experts, depth, width = master_gate.shape
     side = 4
     own, chunks = router_weight.shape[1], 2 * width // LANES
-    stages = ((0, 1), (1, 4), (4, chunks))
+    stages = ((0, 1), (1, 3), (3, chunks))
     anywhere = pl.BlockSpec(memory_space=pl.ANY)
     vmem = pl.BlockSpec(memory_space=pltpu.VMEM)
     dma, pair = pltpu.SemaphoreType.DMA, pltpu.SemaphoreType.DMA((2,))
@@ -284,7 +291,7 @@
     arrived = pl.pallas_call(
         functools.partial(kernel, ep_size, side, stages),
         out_shape=tuple(pltpu.VMEM(*result) for result in results),
-        in_specs=[anywhere, anywhere, vmem, vmem],
+        in_specs=[anywhere] * 4,
         out_specs=[vmem] * 5,
         scratch_shapes=[
             pltpu.VMEM((2, experts, depth, width), jnp.float32),
@@ -295,10 +302,12 @@
             pltpu.VMEM((chunks, experts, depth, LANES), jnp.bfloat16),
             pltpu.VMEM((fsdp, RAW, LANES), jnp.float32),
             pltpu.VMEM((stages[-1][1] - stages[-1][0], LANES), jnp.float32),
+            pltpu.VMEM((own, depth), jnp.float32),
+            pltpu.VMEM((1, depth), jnp.float32),
             pltpu.VMEM((fsdp, own, depth), jnp.bfloat16),
             pltpu.VMEM((ep_size, fsdp, own, depth), jnp.bfloat16),
             dma((4 * experts // PIECE,)), dma, dma((len(stages), 2)), dma((len(stages), 2)),
-            pair, pair, pair, pair, pair, dma, pltpu.SemaphoreType.REGULAR,
+            pair, pair, pair, pair, pair, dma, pltpu.SemaphoreType.REGULAR, pair,
         ],
         compiler_params=pltpu.CompilerParams(
             collective_id=0, has_side_effects=True, vmem_limit_bytes=48 * 2**20

time: 86.3 us -> 85.3 us (0.988)
  Pallas kernels: 85.5 us -> 84.5 us
    pallas_call x1, Pallas kernels: 82.5 us -> 81.6 us  [body(): pl.pallas_call(functools.partial(kernel, ep_size, side, stages), out_shap...]
where the time goes in v4:
time: 85.3 us; the launch traced here: 85.2 us
  Pallas kernels  84.5 us (99%)
    pallas_call x1, Pallas kernels, body(): pl.pallas_call(functools.partial(kernel, ep_size, side, stages), out_shap...  81.6 us
    pallas_call x1, Pallas kernels, body(): pl.pallas_call(place, out_shape=tuple((jax.ShapeDtypeStruct(*result) for...  2.95 us

profile of v4, /device:TPU:0, one launch (start us, length us, event | category | flops | bytes accessed | tf_op | source)
XLA Modules:
  0.0 85.2 jit_solution(444499613892888790)
XLA Ops:
  0.6 81.6 %relayout.1 = (bf16[2048,768]{1,0:T(8,128)(2,1)S(1)}, bf16[2048,768]{1,0:T(8,128)(2,1)S(1)}, f32[1,768]{1,0:T(1,128)S(1)}, f32[1,768]{1,0:T(1,128)S(1)}, bf16[2048,128]{1,0:T(8,128)(2,1)S(1)}) custom-call(f32[16,128,768]{2,1,0:T(8,128)} %gate.1, f32[16,128,768]{2,1,0:T(8,128)} %up.1, f32[16,128]{1,0:T(8,128)} %bitcast.4, f32[1,128]{1,0:T(1,128)} %bitcast.5), custom_call_target="tpu_custom_call" | custom-call | tf_op jit(solution)/shard_map/relayout/pallas_call | solution.py:291
  82.2 3.0 %place.1 = (bf16[2048,768]{1,0:T(8,128)(2,1)}, bf16[2048,768]{1,0:T(8,128)(2,1)}, f32[1,768]{1,0:T(1,128)}, f32[1,768]{1,0:T(1,128)}, bf16[2048,128]{1,0:T(8,128)(2,1)}) custom-call(bf16[2048,768]{1,0:T(8,128)(2,1)S(1)} %get-tuple-element.15.refs_0_, bf16[2048,768]{1,0:T(8,128)(2,1)S(1)} %get-tuple-element.16.refs_1_, ...), custom_call_target="tpu_custom_call" | custom-call | tf_op jit(solution)/shard_map/place/pallas_call | solution.py:317

commit v5 on v4

--- a/solution.py
+++ b/solution.py
@@ -11,7 +11,7 @@
 LANES = 128
 HEAD = 3
 RAW = 16
-PIECE = 4
+PIECE = 8
 ORDER = (
     (2, 2), (2, 1), (1, 2), (2, 3), (3, 2), (1, 1), (3, 3), (1, 3),
     (3, 1), (2, 0), (0, 2), (1, 0), (0, 1), (3, 0), (0, 3),
@@ -257,7 +257,7 @@
     count = (len(refs) - 1) // 2
     copies = []
     for source, target in zip(refs[:count], refs[count : 2 * count]):
-        pieces = 4 if source.shape[0] > 8 else 1
+        pieces = 1
         step = source.shape[0] // pieces
         for k in range(pieces):
             at = pl.ds(k * step, step)

time: 85.3 us -> 85.3 us (level)
  no operation moved by 1% of the time
where the time goes in v5:
time: 85.3 us; the launch traced here: 85.2 us
  Pallas kernels  84.5 us (99%)
    pallas_call x1, Pallas kernels, body(): pl.pallas_call(functools.partial(kernel, ep_size, side, stages), out_shap...  81.5 us
    pallas_call x1, Pallas kernels, body(): pl.pallas_call(place, out_shape=tuple((jax.ShapeDtypeStruct(*result) for...  3.02 us

profile of v5, /device:TPU:0, one launch (start us, length us, event | category | flops | bytes accessed | tf_op | source)
XLA Modules:
  0.0 85.2 jit_solution(18173924109308117178)
XLA Ops:
  0.6 81.5 %relayout.1 = (bf16[2048,768]{1,0:T(8,128)(2,1)S(1)}, bf16[2048,768]{1,0:T(8,128)(2,1)S(1)}, f32[1,768]{1,0:T(1,128)S(1)}, f32[1,768]{1,0:T(1,128)S(1)}, bf16[2048,128]{1,0:T(8,128)(2,1)S(1)}) custom-call(f32[16,128,768]{2,1,0:T(8,128)} %gate.1, f32[16,128,768]{2,1,0:T(8,128)} %up.1, f32[16,128]{1,0:T(8,128)} %bitcast.4, f32[1,128]{1,0:T(1,128)} %bitcast.5), custom_call_target="tpu_custom_call" | custom-call | tf_op jit(solution)/shard_map/relayout/pallas_call | solution.py:291
  82.2 3.0 %place.1 = (bf16[2048,768]{1,0:T(8,128)(2,1)}, bf16[2048,768]{1,0:T(8,128)(2,1)}, f32[1,768]{1,0:T(1,128)}, f32[1,768]{1,0:T(1,128)}, bf16[2048,128]{1,0:T(8,128)(2,1)}) custom-call(bf16[2048,768]{1,0:T(8,128)(2,1)S(1)} %get-tuple-element.15.refs_0_, bf16[2048,768]{1,0:T(8,128)(2,1)S(1)} %get-tuple-element.16.refs_1_, ...), custom_call_target="tpu_custom_call" | custom-call | tf_op jit(solution)/shard_map/place/pallas_call | solution.py:317

commit v6 on v4

--- a/solution.py
+++ b/solution.py
@@ -272,7 +272,7 @@
     experts, depth, width = master_gate.shape
     side = 4
     own, chunks = router_weight.shape[1], 2 * width // LANES
-    stages = ((0, 1), (1, 3), (3, chunks))
+    stages = ((0, 1), (1, 4), (4, chunks))
     anywhere = pl.BlockSpec(memory_space=pl.ANY)
     vmem = pl.BlockSpec(memory_space=pltpu.VMEM)
     dma, pair = pltpu.SemaphoreType.DMA, pltpu.SemaphoreType.DMA((2,))

time: 85.3 us -> 85.2 us (level)
  no operation moved by 1% of the time
where the time goes in v6:
time: 85.2 us; the launch traced here: 85.1 us
  Pallas kernels  84.5 us (99%)
    pallas_call x1, Pallas kernels, body(): pl.pallas_call(functools.partial(kernel, ep_size, side, stages), out_shap...  81.5 us
    pallas_call x1, Pallas kernels, body(): pl.pallas_call(place, out_shape=tuple((jax.ShapeDtypeStruct(*result) for...  2.95 us

profile of v6, /device:TPU:0, one launch (start us, length us, event | category | flops | bytes accessed | tf_op | source)
XLA Modules:
  0.0 85.1 jit_solution(3645920154319262697)
XLA Ops:
  0.6 81.5 %relayout.1 = (bf16[2048,768]{1,0:T(8,128)(2,1)S(1)}, bf16[2048,768]{1,0:T(8,128)(2,1)S(1)}, f32[1,768]{1,0:T(1,128)S(1)}, f32[1,768]{1,0:T(1,128)S(1)}, bf16[2048,128]{1,0:T(8,128)(2,1)S(1)}) custom-call(f32[16,128,768]{2,1,0:T(8,128)} %gate.1, f32[16,128,768]{2,1,0:T(8,128)} %up.1, f32[16,128]{1,0:T(8,128)} %bitcast.4, f32[1,128]{1,0:T(1,128)} %bitcast.5), custom_call_target="tpu_custom_call" | custom-call | tf_op jit(solution)/shard_map/relayout/pallas_call | solution.py:291
  82.2 3.0 %place.1 = (bf16[2048,768]{1,0:T(8,128)(2,1)}, bf16[2048,768]{1,0:T(8,128)(2,1)}, f32[1,768]{1,0:T(1,128)}, f32[1,768]{1,0:T(1,128)}, bf16[2048,128]{1,0:T(8,128)(2,1)}) custom-call(bf16[2048,768]{1,0:T(8,128)(2,1)S(1)} %get-tuple-element.15.refs_0_, bf16[2048,768]{1,0:T(8,128)(2,1)S(1)} %get-tuple-element.16.refs_1_, ...), custom_call_target="tpu_custom_call" | custom-call | tf_op jit(solution)/shard_map/place/pallas_call | solution.py:317
